TPU v7x, 32 devices: a whole 2x2x4 slice. The times are simulated.
32 devices in a mesh: row: 4 (over y, x), col: 8 (over z, core).
Axes of the slice: x: 2, y: 2, z: 4, core: 2. Of those that a mesh axis runs over, the one named last changes fastest.
Arguments:
- pair_states: bfloat16 [1024, 16384], P(None, ('row', 'col')), may hold values from -0.046875 to 0.046875
- screening: bfloat16 [4, 16384, 16384], P(None, 'row', 'col'), may hold values from -6 to 6
- qp_energy: float32 [8], replicated, may hold values from -0.5 to 0.5
- band_energy: float32 [2048], replicated, may hold values from -2 to 2
- band_index: int32 [128], replicated, may hold values from 0 to 2047
- nodes: float32 [4], replicated, may hold values from 0.1 to 2
- node_weights: float32 [4], replicated, may hold values from 0.05 to 1
Outputs:
- contrib: float32 [8, 128], replicated
- sigma: float32 [8], replicated
All inputs are finite; a program needn't handle non-finite values.
Results may differ from a plain program's by a relative error of at most 0.0003.
Values may be sent and summed in bfloat16 or wider, within the bound.
A program may use at most 128 MiB of HBM per device.

v0:
```python
import jax
import jax.numpy as jnp
from jax import lax
from jax.sharding import PartitionSpec as P


def broadcast(block, axis, holder):
    block = jnp.where(lax.axis_index(axis) == holder, block, jnp.zeros_like(block))
    return lax.psum(block, axis)


def shards(pair_states, screening, qp_energy, band_energy, band_index, nodes, node_weights):
    width = screening.shape[2]
    panel = lax.all_gather(pair_states, "col", axis=1, tiled=True)
    images = jnp.einsum("pg,fgc->fpc", panel, screening, preferred_element_type=jnp.float32)
    ratio = lax.axis_size("col") // lax.axis_size("row")
    column = lax.axis_index("col")
    offset = column % ratio * width
    own_piece = lax.dynamic_slice_in_dim(panel, offset, width, 1)
    col_states = broadcast(own_piece, "row", column // ratio)
    partial_value = jnp.sum(images * col_states.astype(jnp.float32)[None, :, :], axis=2)
    table = lax.broadcasted_iota(jnp.int32, (band_index.shape[0], band_energy.shape[0]), 1)
    chosen = jnp.sum(
        jnp.where(band_index[:, None] == table, band_energy[None, :], jnp.float32(0.0)), axis=1
    )
    gap = (qp_energy[:, None] - chosen[None, :]).reshape(-1)
    factor = (
        node_weights[:, None]
        * gap[None, :]
        / (gap[None, :] * gap[None, :] + nodes[:, None] * nodes[:, None])
    )
    flat = lax.psum(jnp.sum(factor * partial_value, axis=0), ("row", "col"))
    contrib = flat.reshape(qp_energy.shape[0], band_index.shape[0])
    sigma = jnp.sum(contrib, axis=1)
    return (contrib, sigma)


def solution(mesh):
    in_specs = (P(None, ("row", "col")), P(None, "row", "col"), P(), P(), P(), P(), P())
    out_specs = (P(), P())
    return jax.shard_map(shards, mesh=mesh, in_specs=in_specs, out_specs=out_specs, check_vma=False)
```

profile of v0, /device:TPU:0, one launch (start us, length us, event | category | flops | bytes accessed | tf_op | source)
XLA Modules:
  0.0 333.2 jit_solution(11457879454940917840)
XLA Ops:
  7.2 0.0 copy-start.8
  7.2 0.0 copy-start.3
  7.2 0.0 copy-start.5
  7.2 0.0 copy-start.4
  7.2 0.0 all-gather.2.cloned.1.call-start
  7.2 0.7 all-gather.2.cloned.1.call-update
  7.9 0.0 all-reduce.2.cloned.1.call-start
  8.0 86.4 %all-gather.2.cloned.1.call-done = bf16[1024,4096]{1,0:T(8,128)(2,1)} async-done(((bf16[1024,512]{1,0:T(8,128)(2,1)}), bf16[1024,4096]{1,0:T(8,128)(2,1)}) %all-gather.2.cloned.1.call-update) | async-done | bytes 8388624 | tf_op jit(solution)/shard_map/all_gather | solution.py:14
  94.4 5.5 %dynamic-slice_select_fusion = bf16[1024,2048]{1,0:T(8,128)(2,1)} fusion(bf16[1024,4096]{1,0:T(8,128)(2,1)} %all-gather.2.cloned.1.call-done, s32[]{:T(128)S(6)} %select_n.30, pred[]{:T(512)S(6)} %eq.15), kind=kLoop, calls=%fused_computation.3 | loop fusion | flops 2097152 | bytes 8388613 | tf_op jit(solution)/shard_map/jit(_where)/select_n | solution.py:8
  99.9 0.0 all-reduce.2.cloned.1.call-update
  99.9 0.0 copy-done.8
  99.9 0.5 mul.43
  100.4 0.0 copy-done.3
  100.4 0.0 copy-done.5
  100.4 0.2 select_reduce_fusion
  100.7 0.0 copy-done.4
  100.7 0.7 fusion.2
  101.4 0.7 subtract_bitcast_fusion
  102.0 100.2 %all-reduce.2.cloned.1.call-done = bf16[1024,2048]{1,0:T(8,128)(2,1)} async-done(((bf16[1024,2048]{1,0:T(8,128)(2,1)}), bf16[1024,2048]{1,0:T(8,128)(2,1)}) %all-reduce.2.cloned.1.call-update) | async-done | bytes 4194320 | tf_op jit(solution)/shard_map/psum | solution.py:9
  202.2 6.9 %copy.12 = f32[1024,2048]{0,1:T(8,128)} copy(bf16[1024,2048]{1,0:T(8,128)(2,1)} %all-reduce.2.cloned.1.call-done) | data formatting | bytes 12582912 | tf_op jit(solution)/shard_map/convert_element_type | solution.py:21
  209.1 77.2 %fusion = f32[4,1024]{1,0:T(4,128)S(1)} fusion(bf16[4,4096,2048]{2,1,0:T(8,128)(2,1)} %param.8, f32[1024,2048]{0,1:T(8,128)} %copy.12, bf16[1024,4096]{1,0:T(8,128)(2,1)} %all-gather.2.cloned.1.call-done), kind=kOutput, calls=%fused_computation.1 | convolution fusion | flops 68736253952 | bytes 83902464 | tf_op jit(solution)/shard_map/pg,fgc->fpc/dot_general | solution.py:15
  286.3 0.1 multiply_reduce_fusion
  286.4 39.3 %psum.15 = f32[8,128]{1,0:T(8,128)S(1)} all-reduce(f32[8,128]{1,0:T(8,128)S(1)} %bitcast.13), channel_id=1, replica_groups=mesh['row'=4,'col'=8] {'row','col'}, use_global_device_ids=true, to_apply=%region_4.5 | all-reduce | flops 1024 | bytes 8192 | tf_op jit(solution)/shard_map/psum | solution.py:32
  325.8 0.6 reduce_sum.39
  (10 shorter events, 0.0 us)
Async XLA Ops:
  7.2 92.8 %copy-start.8 = (f32[4]{0:T(128)S(1)}, f32[4]{0:T(128)}, u32[]{:S(2)}) copy-start(f32[4]{0:T(128)} %param.12) | copy-start | bytes 52
  7.2 93.3 %copy-start.3 = (f32[2048]{0:T(1024)S(1)}, f32[2048]{0:T(1024)}, u32[]{:S(2)}) copy-start(f32[2048]{0:T(1024)} %param.10) | copy-start | bytes 24580
  7.2 93.3 %copy-start.5 = (s32[128]{0:T(128)S(1)}, s32[128]{0:T(128)}, u32[]{:S(2)}) copy-start(s32[128]{0:T(128)} %param.11) | copy-start | bytes 1540
  7.2 93.5 %copy-start.4 = (f32[8]{0:T(128)S(1)}, f32[8]{0:T(128)}, u32[]{:S(2)}) copy-start(f32[8]{0:T(128)} %param.9) | copy-start | bytes 100
  7.2 87.2 %all-gather.2.cloned.1.call-start = ((), (), s32[]{:S(2)}) async-start(), calls=%async_computation | async-start | bytes 9437184 | tf_op jit(solution)/shard_map/all_gather | solution.py:14
  7.9 194.2 %all-reduce.2.cloned.1.call-start = ((), (), s32[]{:S(2)}) async-start(), calls=%async_computation.1 | async-start | bytes 8388608 | tf_op jit(solution)/shard_map/psum | solution.py:9
  209.0 77.3 %copy-start.1 = (f32[1024]{0:T(1024)S(1)}, f32[1024]{0:T(1024)}, u32[]{:S(2)}) copy-start(f32[1024]{0:T(1024)} %fusion.2) | copy-start | bytes 12292
  209.0 77.3 %copy-start.2 = (f32[1024]{0:T(1024)S(1)}, f32[1024]{0:T(1024)}, u32[]{:S(2)}) copy-start(f32[1024]{0:T(1024)} %subtract_bitcast_fusion) | copy-start | bytes 12292
  209.0 77.3 %copy-start.6 = (f32[4]{0:T(128)S(1)}, f32[4]{0:T(128)}, u32[]{:S(2)}) copy-start(f32[4]{0:T(128)} %param.13) | copy-start | bytes 52
  209.0 77.3 %copy-start.7 = (f32[4]{0:T(128)S(1)}, f32[4]{0:T(128)}, u32[]{:S(2)}) copy-start(f32[4]{0:T(128)} %mul.43) | copy-start | bytes 52
  325.8 0.6 copy-start
Sparse Core Ops, SparseCore 0:
  9.6 84.7 all-gather.1
  100.0 102.0 all-reduce.1
where the time goes:
time: 334 us; the launch traced here: 333 us
  waiting for transfers between devices  187 us (56%)
  matrix products  77.2 us (23%)
  blocking collectives  39.3 us (12%)
  between operations  14.2 us (4%)
  other arithmetic  8.28 us (2%)
  local copies, waits for them, and re-layouts  6.9 us (2%)
    psum x1, waiting for transfers between devices, broadcast(): return lax.psum(block, axis)  100 us
    all_gather x1, waiting for transfers between devices, shards(): panel = lax.all_gather(pair_states, 'col', axis=1, tiled=True)  86.4 us
    dot_general x1, matrix products, shards(): jnp.einsum('pg,fgc->fpc', panel, screening, preferred_element_type=jnp.fl...  77.2 us
    psum x1, blocking collectives, shards(): flat = lax.psum(jnp.sum(factor * partial_value, axis=0), ('row', 'col'))  39.3 us
    convert_element_type x1, local copies, waits for them, and re-layouts, shards(): col_states.astype(jnp.float32)[None, :, :]  6.86 us
  transfers between devices with their start and end apart: 2, of which 2 were waited for; matrix products, arithmetic and copies ran while one was open for 1% of the time, Pallas kernels for 0%

commit v1 on v0

--- a/solution.py
+++ b/solution.py
@@ -6,7 +6,7 @@
 
 def broadcast(block, axis, holder):
     block = jnp.where(lax.axis_index(axis) == holder, block, jnp.zeros_like(block))
-    return lax.psum(block, axis)
+    return jnp.sum(lax.all_gather(block, axis), axis=0)
 
 
 def shards(pair_states, screening, qp_energy, band_energy, band_index, nodes, node_weights):

time: 334 us -> 399 us (1.19)
  waiting for transfers between devices: 187 us -> 241 us
  other arithmetic: 8.28 us -> 20.4 us
    all_gather x0 -> x1, waiting for transfers between devices: none -> 154 us  [broadcast(): return jnp.sum(lax.all_gather(block, axis), axis=0)]
    psum x1 -> x0, waiting for transfers between devices: 100 us -> none  [broadcast(): return lax.psum(block, axis)]
    reduce_sum x0 -> x1, other arithmetic: none -> 12.1 us  [broadcast(): return jnp.sum(lax.all_gather(block, axis), axis=0)]
where the time goes in v1:
time: 399 us
  waiting for transfers between devices  241 us (60%)
  matrix products  77.2 us (19%)
  blocking collectives  39.3 us (10%)
  other arithmetic  20.4 us (5%)
  between operations  14.2 us (4%)
  local copies, waits for them, and re-layouts  6.9 us (2%)
    all_gather x1, waiting for transfers between devices, broadcast(): return jnp.sum(lax.all_gather(block, axis), axis=0)  154 us
    all_gather x1, waiting for transfers between devices, shards(): panel = lax.all_gather(pair_states, 'col', axis=1, tiled=True)  86.4 us
    dot_general x1, matrix products, shards(): jnp.einsum('pg,fgc->fpc', panel, screening, preferred_element_type=jnp.fl...  77.2 us
    psum x1, blocking collectives, shards(): flat = lax.psum(jnp.sum(factor * partial_value, axis=0), ('row', 'col'))  39.3 us
    reduce_sum x1, other arithmetic, broadcast(): return jnp.sum(lax.all_gather(block, axis), axis=0)  12.1 us
  transfers between devices with their start and end apart: 2, of which 2 were waited for; matrix products, arithmetic and copies ran while one was open for 1% of the time, Pallas kernels for 0%

profile of v1, /device:TPU:0, one launch (start us, length us, event | category | flops | bytes accessed | tf_op | source)
XLA Modules:
  0.0 399.0 jit_solution(7528455744867752103)
XLA Ops:
  7.2 0.0 copy-start.8
  7.2 0.0 copy-start.3
  7.2 0.0 copy-start.5
  7.2 0.0 copy-start.4
  7.2 0.0 all-gather.4.cloned.1.call-start
  7.2 0.7 all-gather.4.cloned.1.call-update
  7.9 0.0 all-gather.6.cloned.1.call-start
  8.0 86.4 %all-gather.4.cloned.1.call-done = bf16[1024,4096]{1,0:T(8,128)(2,1)} async-done(((bf16[1024,512]{1,0:T(8,128)(2,1)}), bf16[1024,4096]{1,0:T(8,128)(2,1)}) %all-gather.4.cloned.1.call-update) | async-done | bytes 8388624 | tf_op jit(solution)/shard_map/all_gather | solution.py:14
  94.4 5.5 %dynamic-slice_select_fusion = bf16[1024,2048]{1,0:T(8,128)(2,1)} fusion(bf16[1024,4096]{1,0:T(8,128)(2,1)} %all-gather.4.cloned.1.call-done, s32[]{:T(128)S(6)} %select_n.30, pred[]{:T(512)S(6)} %eq.15), kind=kLoop, calls=%fused_computation.3 | loop fusion | flops 2097152 | bytes 8388613 | tf_op jit(solution)/shard_map/jit(_where)/select_n | solution.py:8
  99.9 0.0 all-gather.6.cloned.1.call-update
  99.9 0.0 copy-done.8
  99.9 0.5 mul.43
  100.4 0.0 copy-done.3
  100.4 0.2 select_reduce_fusion
  100.7 0.7 fusion.2
  101.4 0.7 subtract_bitcast_fusion
  102.0 153.8 %all-gather.6.cloned.1.call-done = bf16[4096,2048]{1,0:T(8,128)(2,1)} async-done(((bf16[1024,2048]{1,0:T(8,128)(2,1)}), bf16[4096,2048]{1,0:T(8,128)(2,1)}) %all-gather.6.cloned.1.call-update) | async-done | bytes 16777232 | tf_op jit(solution)/shard_map/all_gather | solution.py:9
  255.8 12.1 %reduce_sum.49 = bf16[1024,2048]{1,0:T(8,128)(2,1)} reduce(bf16[4,1024,2048]{2,1,0:T(8,128)(2,1)} %bitcast.14, bf16[]{:T(256)} %constant.41.clone.1), dimensions={0}, to_apply=%region_1.2 | reduce | flops 6291456 | bytes 20971522 | tf_op jit(solution)/shard_map/reduce_sum | solution.py:9
  267.9 6.9 %copy.13 = f32[1024,2048]{0,1:T(8,128)} copy(bf16[1024,2048]{1,0:T(8,128)(2,1)} %reduce_sum.49) | data formatting | bytes 12582912 | tf_op jit(solution)/shard_map/convert_element_type | solution.py:21
  274.8 77.2 %fusion = f32[4,1024]{1,0:T(4,128)S(1)} fusion(bf16[4,4096,2048]{2,1,0:T(8,128)(2,1)} %param.8, f32[1024,2048]{0,1:T(8,128)} %copy.13, bf16[1024,4096]{1,0:T(8,128)(2,1)} %all-gather.4.cloned.1.call-done), kind=kOutput, calls=%fused_computation.1 | convolution fusion | flops 68736253952 | bytes 83902464 | tf_op jit(solution)/shard_map/pg,fgc->fpc/dot_general | solution.py:15
  352.1 0.1 multiply_reduce_fusion
  352.2 39.3 %psum.7 = f32[8,128]{1,0:T(8,128)S(1)} all-reduce(f32[8,128]{1,0:T(8,128)S(1)} %bitcast.15), channel_id=1, replica_groups=mesh['row'=4,'col'=8] {'row','col'}, use_global_device_ids=true, to_apply=%region_4.5 | all-reduce | flops 1024 | bytes 8192 | tf_op jit(solution)/shard_map/psum | solution.py:32
  391.5 0.6 reduce_sum.52
  392.1 0.0 copy-done
  (11 shorter events, 0.0 us)
Async XLA Ops:
  7.2 92.8 %copy-start.8 = (f32[4]{0:T(128)S(1)}, f32[4]{0:T(128)}, u32[]{:S(2)}) copy-start(f32[4]{0:T(128)} %param.12) | copy-start | bytes 52
  7.2 93.3 %copy-start.3 = (f32[2048]{0:T(1024)S(1)}, f32[2048]{0:T(1024)}, u32[]{:S(2)}) copy-start(f32[2048]{0:T(1024)} %param.10) | copy-start | bytes 24580
  7.2 93.3 %copy-start.5 = (s32[128]{0:T(128)S(1)}, s32[128]{0:T(128)}, u32[]{:S(2)}) copy-start(s32[128]{0:T(128)} %param.11) | copy-start | bytes 1540
  7.2 93.5 %copy-start.4 = (f32[8]{0:T(128)S(1)}, f32[8]{0:T(128)}, u32[]{:S(2)}) copy-start(f32[8]{0:T(128)} %param.9) | copy-start | bytes 100
  7.2 87.2 %all-gather.4.cloned.1.call-start = ((), (), s32[]{:S(2)}) async-start(), calls=%async_computation | async-start | bytes 9437184 | tf_op jit(solution)/shard_map/all_gather | solution.py:14
  7.9 247.9 %all-gather.6.cloned.1.call-start = ((), (), s32[]{:S(2)}) async-start(), calls=%async_computation.1 | async-start | bytes 20971520 | tf_op jit(solution)/shard_map/all_gather | solution.py:9
  274.8 77.3 %copy-start.1 = (f32[1024]{0:T(1024)S(1)}, f32[1024]{0:T(1024)}, u32[]{:S(2)}) copy-start(f32[1024]{0:T(1024)} %fusion.2) | copy-start | bytes 12292
  274.8 77.3 %copy-start.2 = (f32[1024]{0:T(1024)S(1)}, f32[1024]{0:T(1024)}, u32[]{:S(2)}) copy-start(f32[1024]{0:T(1024)} %subtract_bitcast_fusion) | copy-start | bytes 12292
  274.8 77.3 %copy-start.6 = (f32[4]{0:T(128)S(1)}, f32[4]{0:T(128)}, u32[]{:S(2)}) copy-start(f32[4]{0:T(128)} %param.13) | copy-start | bytes 52
  274.8 77.3 %copy-start.7 = (f32[4]{0:T(128)S(1)}, f32[4]{0:T(128)}, u32[]{:S(2)}) copy-start(f32[4]{0:T(128)} %mul.43) | copy-start | bytes 52
  391.5 0.6 copy-start
Sparse Core Ops, SparseCore 0:
  9.6 84.7 all-gather.3
  100.0 155.7 all-gather.5
